TPU v7x, 256 devices: a whole 4x4x8 slice. The times are simulated.
256 devices in a mesh: zero: 16 (over z, core), cols: 4 (over y), ens: 4 (over x).
Axes of the slice: x: 4, y: 4, z: 8, core: 2. Of those that a mesh axis runs over, the one named last changes fastest.
Arguments:
- weight_gate: float32 [8192, 8192], P(('ens', 'zero'), 'cols'), parts along dimension 0, may hold values from -0.1875 to 0.1875
- moment_gate: float32 [8192, 8192], P(('ens', 'zero'), 'cols'), parts along dimension 0, may hold values from -0.125 to 0.125
- square_gate: float32 [8192, 8192], P(('ens', 'zero'), 'cols'), parts along dimension 0, may hold values from -0.125 to 0.125
- weight_up: float32 [8192, 8192], P(('ens', 'zero'), 'cols'), parts along dimension 0, may hold values from -0.1875 to 0.1875
- moment_up: float32 [8192, 8192], P(('ens', 'zero'), 'cols'), parts along dimension 0, may hold values from -0.125 to 0.125
- square_up: float32 [8192, 8192], P(('ens', 'zero'), 'cols'), parts along dimension 0, may hold values from -0.125 to 0.125
- norm_gain: float32 [8192], P(('ens', 'zero')), parts along dimension 0, may hold values from 0.25 to 1.75
Outputs:
- ready_gate: bfloat16 [8192, 8192], P('ens', 'cols'), parts along dimension 0
- ready_up: bfloat16 [8192, 8192], P('ens', 'cols'), parts along dimension 0
- factor_gate: float32 [32768], P(('ens', 'cols')), parts along dimension 0
- factor_up: float32 [32768], P(('ens', 'cols')), parts along dimension 0
There are 4 independent parts, one for each index of `ens`. A program takes and returns all parts, laid end to end along the dimension named above; each array names one. Nothing has to cross between parts.
All inputs are finite; a program needn't handle non-finite values. Where the computation divides by a largest or mean magnitude, that divisor is 1e-20 or more.
Results may differ from a plain program's by a relative error of at most 0.001.
Values may be sent and summed in bfloat16 or wider, within the bound.
A program may use at most 128 MiB of HBM per device.

v0:
```python
import jax
import jax.numpy as jnp
from jax import lax
from jax.sharding import PartitionSpec as P

learn_rate = 0.2
hold_rate = 0.9


def from_everyone(x, axis):
    length = lax.axis_size(axis)
    return lax.all_to_all(jnp.broadcast_to(x[None], (length, *x.shape)), axis, 0, 0, tiled=True)


def over_copies(x, axis):
    everything = from_everyone(x, axis)
    return jnp.max(everything, axis=0)


def together(arrays, axis):
    ravelled, at, outs = (jnp.concatenate([a.reshape(-1) for a in arrays]), 0, [])
    so_far = over_copies(ravelled, axis)
    for a in arrays:
        outs.append(so_far[at : at + a.size].reshape(a.shape))
        at += a.size
    return tuple(outs)


def side_by_side(arrays, axis, dim, along):
    ends, at = ([], 0)
    for a in arrays[:-1]:
        at += a.shape[along]
        ends.append(at)
    both = jnp.concatenate(arrays, axis=along)
    return tuple(jnp.split(lax.all_gather(both, axis, axis=dim, tiled=True), ends, axis=along))


def per_device(weight_gate, moment_gate, square_gate, weight_up, moment_up, square_up, norm_gain):
    hold_gate = hold_rate * moment_gate + square_gate
    latest_gate = weight_gate - learn_rate * hold_gate
    hold_up = hold_rate * moment_up + square_up
    latest_up = weight_up - learn_rate * hold_up
    latest_gained_gate = latest_gate * norm_gain[:, None]
    latest_gained_up = latest_up * norm_gain[:, None]
    factor_gate, factor_up = together(
        (jnp.max(jnp.abs(latest_gained_gate), axis=0), jnp.max(jnp.abs(latest_gained_up), axis=0)),
        "zero",
    )
    narrow_gate, narrow_up = (
        (latest_gained_gate / factor_gate).astype(jnp.bfloat16),
        (latest_gained_up / factor_up).astype(jnp.bfloat16),
    )
    ready_gate, ready_up = side_by_side((narrow_gate, narrow_up), "zero", 0, 1)
    return (ready_gate, ready_up, factor_gate, factor_up)


def solution(mesh):
    placed = (
        P(("ens", "zero"), "cols"),
        P(("ens", "zero"), "cols"),
        P(("ens", "zero"), "cols"),
        P(("ens", "zero"), "cols"),
        P(("ens", "zero"), "cols"),
        P(("ens", "zero"), "cols"),
        P(("ens", "zero")),
    )
    return jax.shard_map(
        per_device,
        mesh=mesh,
        in_specs=placed,
        out_specs=(P("ens", "cols"), P("ens", "cols"), P(("ens", "cols")), P(("ens", "cols"))),
        check_vma=False,
    )
```

profile of v0, /device:TPU:1, one launch (start us, length us, event | category | flops | bytes accessed | tf_op | source)
XLA Modules:
  0.0 145.1 jit_solution(5447473150164090124)
XLA Ops:
  7.2 0.0 all-gather.2.cloned.1.call-start
  7.2 3.3 %abs_reduce_fusion.1 = (f32[2048]{0:T(1024)S(1)}, f32[128,2048]{1,0:T(8,128)S(1)}, f32[2048]{0:T(1024)S(1)}, f32[128,2048]{1,0:T(8,128)S(1)}) fusion(f32[128]{0:T(128)} %param.13, f32[128,2048]{1,0:T(8,128)} %param.7, f32[128,2048]{1,0:T(8,128)} %param.9, f32[128,2048]{1,0:T(8,128)} %param.8, f32[128,2048]{1,0:T(8,128)} %param.10, f32[128,2048]{1,0:T(8,128)} %param.12, ...), kind=kLoop, calls=%fused_computation.5 | loop fusion | flops 3665920 | bytes 8405504 | tf_op jit(solution)/shard_map/reduce_max | solution.py:46
  10.5 0.2 broadcast_in_dim.2
  10.7 21.4 %all_to_all.6 = f32[16,1,4096]{2,1,0:T(1,128)S(1)} all-to-all(f32[16,1,4096]{2,1,0:T(1,128)S(1)} %broadcast_in_dim.2), channel_id=1, replica_groups=mesh['zero'=16,'cols'=4,'ens'=4] {'zero'}, dimensions={0} | all-to-all | bytes 524288 | tf_op jit(solution)/shard_map/all_to_all | solution.py:12
  32.1 0.2 reduce_max.29
  32.3 0.0 copy-start
  32.3 0.0 copy-start.1
  32.3 0.2 divide_convert_fusion
  32.5 1.1 pad_maximum_fusion
  33.6 0.0 all-gather.2.cloned.1.call-update
  33.6 92.7 %all-gather.2.cloned.1.call-done = bf16[2048,4096]{1,0:T(8,128)(2,1)} async-done(((bf16[128,4096]{1,0:T(8,128)(2,1)}), bf16[2048,4096]{1,0:T(8,128)(2,1)}) %all-gather.2.cloned.1.call-update) | async-done | bytes 16777232 | tf_op jit(solution)/shard_map/all_gather | solution.py:35
  126.3 11.9 %fusion = (bf16[2048,2048]{1,0:T(8,128)(2,1)}, bf16[2048,2048]{1,0:T(8,128)(2,1)}) fusion(bf16[2048,4096]{1,0:T(8,128)(2,1)} %all-gather.2.cloned.1.call-done), kind=kLoop, calls=%fused_computation.8 | loop fusion | bytes 33554432 | tf_op jit(solution)/shard_map/split | solution.py:35
  138.2 0.0 copy-done
  138.2 0.0 copy-done.1
  (2 shorter events, 0.0 us)
Async XLA Ops:
  7.2 119.1 %all-gather.2.cloned.1.call-start = ((), (), s32[]{:S(2)}) async-start(), calls=%async_computation.1 | async-start | bytes 17825792 | tf_op jit(solution)/shard_map/all_gather | solution.py:35
  32.3 106.0 %copy-start = (f32[2048]{0:T(1024)}, f32[2048]{0:T(1024)S(1)}, u32[]{:S(2)}) copy-start(f32[2048]{0:T(1024)S(1)} %get-tuple-element.10) | copy-start | bytes 24580
  32.3 106.0 %copy-start.1 = (f32[2048]{0:T(1024)}, f32[2048]{0:T(1024)S(1)}, u32[]{:S(2)}) copy-start(f32[2048]{0:T(1024)S(1)} %get-tuple-element.11) | copy-start | bytes 24580
Sparse Core Ops, SparseCore 0:
  33.7 92.5 all-gather.1
where the time goes:
time: 145 us
  waiting for transfers between devices  92.7 us (64%)
  blocking collectives  21.4 us (15%)
  between operations  14.1 us (10%)
  local copies, waits for them, and re-layouts  12.2 us (8%)
  other arithmetic  4.73 us (3%)
    all_gather x1, waiting for transfers between devices, side_by_side(): lax.all_gather(both, axis, axis=dim, tiled=True)  92.7 us
    all_to_all x1, blocking collectives, from_everyone(): lax.all_to_all(jnp.broadcast_to(x[None], (length, *x.shape)), axis, 0, 0,...  21.4 us
    split x1, local copies, waits for them, and re-layouts, side_by_side(): jnp.split(lax.all_gather(both, axis, axis=dim, tiled=True), ends, axis=al...  11.9 us
    reduce_max x1, other arithmetic, per_device(): jnp.max(jnp.abs(latest_gained_gate), axis=0)  3.3 us
  transfers between devices with their start and end apart: 1, of which 1 were waited for; matrix products, arithmetic and copies ran while one was open for 0% of the time, Pallas kernels for 0%

commit v1 on v0

v1 whole, which is shorter than its diff:
```python
import jax
import jax.numpy as jnp
from jax import lax
from jax.experimental import pallas as pl
from jax.experimental.pallas import tpu as pltpu
from jax.sharding import PartitionSpec as P

learn_rate = 0.2
hold_rate = 0.9
MESH = pl.DeviceIdType.MESH
LANES = 128
GROUP = 1024
PIECE = 512
CW, CCW = 0, 1


def gather_kernel(
    wg, mg, sg, wu, mu, su, gain_ref, out, fac,
    w_buf, m_buf, s_buf, gain_b, mx_own, mx_pair, mx_comb, mx_all, recip,
    load_sem, ring_send, ring_recv, pair_send, pair_recv, mxp_send, mxp_recv, mx_send, mx_recv,
):
    rows, cols = wg.shape
    groups = cols // GROUP
    n_groups = 2 * groups
    per_group = GROUP // PIECE
    n_pieces = n_groups * per_group
    tiles = GROUP // LANES
    chips = lax.axis_size("zero") // 2

    me = lax.axis_index("zero")
    chip, core = me // 2, me % 2

    def peer(step):
        return {"zero": lax.rem(chip + step + 2 * chips, chips) * 2 + core}

    partner = {"zero": chip * 2 + (1 - core)}

    def loads(g):
        a, c = divmod(g, groups)
        span = pl.ds(c * GROUP, GROUP)
        dst = pl.ds(g * GROUP, GROUP)
        srcs = ((wg, mg, sg), (wu, mu, su))[a]
        return [
            pltpu.make_async_copy(src.at[:, span], buf.at[:, dst], load_sem.at[g, i])
            for i, (src, buf) in enumerate(zip(srcs, (w_buf, m_buf, s_buf)))
        ]

    for g in range(n_groups):
        for copy in loads(g):
            copy.start()

    barrier = pltpu.get_barrier_semaphore()
    pl.semaphore_signal(barrier, inc=1, device_id=partner, device_id_type=MESH)
    for step in (4, 3, 5, 2, 6, 1, 7):
        pl.semaphore_signal(barrier, inc=1, device_id=peer(step), device_id_type=MESH)

    gain_b[...] = jnp.broadcast_to(gain_ref[...], (rows, rows)).T

    for g in range(n_groups):
        for copy in loads(g):
            copy.wait()

        def update(j, _, g=g):
            span = pl.ds(pl.multiple_of(g * GROUP + j * LANES, LANES), LANES)
            hold = hold_rate * m_buf[:, span] + s_buf[:, span]
            gained = (w_buf[:, span] - learn_rate * hold) * gain_b[...]
            w_buf[:, span] = gained
            mx_own[g, pl.ds(j, 1), :] = jnp.max(jnp.abs(gained), axis=0, keepdims=True)
            return 0

        lax.fori_loop(0, tiles, update, 0)

    pl.semaphore_wait(barrier, chips)

    pair_max = pltpu.make_async_remote_copy(
        src_ref=mx_own, dst_ref=mx_pair, send_sem=mxp_send, recv_sem=mxp_recv, device_id=partner, device_id_type=MESH
    )
    pair_max.start()
    pair_max.wait()
    mx_comb[...] = jnp.maximum(mx_own[...], mx_pair[...])

    def max_copy(g, step):
        return pltpu.make_async_remote_copy(
            src_ref=mx_comb.at[g], dst_ref=mx_all.at[g, step - 1], send_sem=mx_send.at[g, step - 1],
            recv_sem=mx_recv.at[g, step - 1], device_id=peer(step), device_id_type=MESH,
        )

    for g in range(n_groups):
        for step in (4, 3, 5, 2, 6, 1, 7):
            max_copy(g, step).start()

    def where(owner, k):
        a = k // (n_pieces // 2)
        c = k % (n_pieces // 2)
        return (
            a,
            pl.ds(pl.multiple_of(owner * rows, rows), rows),
            pl.ds(pl.multiple_of(c * PIECE, PIECE), PIECE),
        )

    def ring_copy(way, hop, k):
        owner = lax.rem(chip + (2 * chips - hop if way == CW else hop), chips) * 2 + core
        ref = out.at[where(owner, k)]
        return pltpu.make_async_remote_copy(
            src_ref=ref, dst_ref=ref, send_sem=ring_send.at[way, hop * n_pieces + k],
            recv_sem=ring_recv.at[way, hop * n_pieces + k],
            device_id=peer(1 if way == CW else -1), device_id_type=MESH,
        )

    def ring_wait(way, hop, k):
        ring_copy(way, hop, k).wait_recv()

    def pair_copy(way, hop, k):
        owner = lax.rem(chip + (2 * chips - hop if way == CW else hop), chips) * 2 + core
        ref = out.at[where(owner, k)]
        slot = (way * 4 + hop) * n_pieces + k
        return pltpu.make_async_remote_copy(
            src_ref=ref, dst_ref=ref, send_sem=pair_send.at[slot], recv_sem=pair_recv.at[slot],
            device_id=partner, device_id_type=MESH,
        )

    my_rows = pl.ds(pl.multiple_of(me * rows, rows), rows)
    for g in range(n_groups):
        a, c = divmod(g, groups)
        top = mx_comb[g]
        for step in range(1, chips):
            max_copy(g, step).wait_recv()
            top = jnp.maximum(top, mx_all[g, step - 1])
        fac[a, pl.ds(c * tiles, tiles), :] = top
        recip[...] = 1.0 / top

        for h in range(per_group):

            def scale(j, _, g=g, a=a, c=c, h=h):
                t = h * (PIECE // LANES) + j
                src = pl.ds(pl.multiple_of(g * GROUP + t * LANES, LANES), LANES)
                dst = pl.ds(pl.multiple_of(c * GROUP + t * LANES, LANES), LANES)
                out[a, my_rows, dst] = (w_buf[:, src] * recip[pl.ds(t, 1), :]).astype(jnp.bfloat16)
                return 0

            lax.fori_loop(0, PIECE // LANES, scale, 0)
            k = g * per_group + h
            ring_copy(CW, 0, k).start()
            ring_copy(CCW, 0, k).start()
            pair_copy(CW, 0, k).start()

    def both(i, _):
        hop, k = i // n_pieces, i % n_pieces
        for way in (CW, CCW):
            ring_wait(way, hop, k)
            ring_copy(way, hop + 1, k).start()
            pair_copy(way, hop + 1, k).start()
        return 0

    lax.fori_loop(0, 2 * n_pieces, both, 0)

    def third(i, _):
        for way, k in ((CW, 2 * i), (CCW, 2 * i), (CW, 2 * i + 1), (CCW, 2 * i + 1)):
            ring_wait(way, 2, k)
        for way, k in ((CW, 2 * i), (CCW, 2 * i + 1)):
            ring_copy(way, 3, k).start()
        for way, k in ((CW, 2 * i), (CCW, 2 * i), (CW, 2 * i + 1), (CCW, 2 * i + 1)):
            pair_copy(way, 3, k).start()
        return 0

    lax.fori_loop(0, n_pieces // 2, third, 0)

    def last_pair(way, k):
        owner = lax.rem(chip + chips // 2, chips) * 2 + core
        ref = out.at[where(owner, k)]
        slot = 4 * n_pieces + k
        return pltpu.make_async_remote_copy(
            src_ref=ref, dst_ref=ref, send_sem=pair_send.at[slot], recv_sem=pair_recv.at[slot],
            device_id=partner, device_id_type=MESH,
        )

    def fourth(i, _):
        for way, k in ((CW, 2 * i), (CCW, 2 * i + 1)):
            ring_wait(way, 3, k)
            last_pair(way, k).start()
        return 0

    lax.fori_loop(0, n_pieces // 2, fourth, 0)

    def drain(i, _):
        hop, k = i // n_pieces, i % n_pieces
        for way in (CW, CCW):
            ring_copy(way, hop, k).wait_send()
            pair_copy(way, hop + 1, k).wait()
        return 0

    lax.fori_loop(0, 3 * n_pieces, drain, 0)

    def drain_last(i, _):
        for way, k in ((CW, 2 * i), (CCW, 2 * i + 1)):
            ring_copy(way, 3, k).wait_send()
            last_pair(way, k).wait()
            pair_copy(CW, 0, k).wait()
        return 0

    lax.fori_loop(0, n_pieces // 2, drain_last, 0)
    for g in range(n_groups):
        for step in range(1, chips):
            max_copy(g, step).wait_send()


def write_kernel(full, fac, gate, up, fac_gate, fac_up, sem, fac_sem):
    rows = full.shape[1]
    pieces = sem.shape[1]
    step = rows // pieces

    def copies():
        for a, (dst, small) in enumerate(((gate, fac_gate), (up, fac_up))):
            yield pltpu.make_async_copy(fac.at[a], small, fac_sem.at[a])
            for i in range(pieces):
                span = pl.ds(i * step, step)
                yield pltpu.make_async_copy(full.at[a, span], dst.at[span], sem.at[a, i])

    for copy in copies():
        copy.start()
    for copy in copies():
        copy.wait()


def per_device(weight_gate, moment_gate, square_gate, weight_up, moment_up, square_up, norm_gain):
    rows, cols = weight_gate.shape
    n = lax.axis_size("zero")
    chips = n // 2
    n_groups = 2 * cols // GROUP
    n_pieces = 2 * cols // PIECE
    hbm = pl.BlockSpec(memory_space=pltpu.HBM)
    vmem = pl.BlockSpec(memory_space=pltpu.VMEM)
    stored = (weight_gate, moment_gate, square_gate, weight_up, moment_up, square_up)
    stored = tuple(pltpu.with_memory_space_constraint(x, pltpu.HBM) for x in stored)
    full, fac = pl.pallas_call(
        gather_kernel,
        name="ring",
        out_shape=(
            pltpu.VMEM((2, n * rows, cols), jnp.bfloat16),
            pltpu.VMEM((2, cols // LANES, LANES), jnp.float32),
        ),
        in_specs=[hbm] * 6 + [vmem],
        out_specs=(vmem, vmem),
        scratch_shapes=[
            pltpu.VMEM((rows, 2 * cols), jnp.float32),
            pltpu.VMEM((rows, 2 * cols), jnp.float32),
            pltpu.VMEM((rows, 2 * cols), jnp.float32),
            pltpu.VMEM((rows, LANES), jnp.float32),
            pltpu.VMEM((n_groups, GROUP // LANES, LANES), jnp.float32),
            pltpu.VMEM((n_groups, GROUP // LANES, LANES), jnp.float32),
            pltpu.VMEM((n_groups, GROUP // LANES, LANES), jnp.float32),
            pltpu.VMEM((n_groups, chips - 1, GROUP // LANES, LANES), jnp.float32),
            pltpu.VMEM((GROUP // LANES, LANES), jnp.float32),
            pltpu.SemaphoreType.DMA((n_groups, 3)),
            pltpu.SemaphoreType.DMA((2, 4 * n_pieces)),
            pltpu.SemaphoreType.DMA((2, 4 * n_pieces)),
            pltpu.SemaphoreType.DMA((8 * n_pieces,)),
            pltpu.SemaphoreType.DMA((8 * n_pieces,)),
            pltpu.SemaphoreType.DMA,
            pltpu.SemaphoreType.DMA,
            pltpu.SemaphoreType.DMA((n_groups, chips - 1)),
            pltpu.SemaphoreType.DMA((n_groups, chips - 1)),
        ],
        compiler_params=pltpu.CompilerParams(
            collective_id=0, has_side_effects=True, vmem_limit_bytes=16 * 1024 * 1024
        ),
    )(*stored, norm_gain.reshape(1, rows))
    full, fac = (pltpu.with_memory_space_constraint(x, pltpu.VMEM) for x in (full, fac))
    gate, up, fac_gate, fac_up = pl.pallas_call(
        write_kernel,
        name="write",
        out_shape=(
            jax.ShapeDtypeStruct((n * rows, cols), jnp.bfloat16),
            jax.ShapeDtypeStruct((n * rows, cols), jnp.bfloat16),
            jax.ShapeDtypeStruct((cols // LANES, LANES), jnp.float32),
            jax.ShapeDtypeStruct((cols // LANES, LANES), jnp.float32),
        ),
        in_specs=[pl.BlockSpec(memory_space=pl.ANY)] * 2,
        out_specs=(hbm,) * 4,
        scratch_shapes=[pltpu.SemaphoreType.DMA((2, 8)), pltpu.SemaphoreType.DMA((2,))],
        compiler_params=pltpu.CompilerParams(vmem_limit_bytes=1024 * 1024),
    )(full, fac)
    return gate, up, fac_gate.reshape(cols), fac_up.reshape(cols)


def solution(mesh):
    placed = (P(("ens", "zero"), "cols"),) * 6 + (P(("ens", "zero")),)
    return jax.shard_map(
        per_device,
        mesh=mesh,
        in_specs=placed,
        out_specs=(P("ens", "cols"), P("ens", "cols"), P(("ens", "cols")), P(("ens", "cols"))),
        check_vma=False,
    )
```

time: 145 us -> 106 us (0.73)
  Pallas kernels: 0 us -> 105 us
  waiting for transfers between devices: 92.7 us -> 0 us
  blocking collectives: 21.4 us -> 0 us
  between operations: 14.1 us -> 0.65 us
  local copies, waits for them, and re-layouts: 12.2 us -> 0.65 us
  other arithmetic: 4.73 us -> 0 us
    pallas_call x0 -> x2, Pallas kernels: none -> 105 us  [the longest x1 98.9 us: per_device(): pl.pallas_call(gather_kernel, name='ring', out_shape=(pltpu.VMEM((2, n *...]
    all_gather x1 -> x0, waiting for transfers between devices: 92.7 us -> none  [side_by_side(): lax.all_gather(both, axis, axis=dim, tiled=True)]
    all_to_all x1 -> x0, blocking collectives: 21.4 us -> none  [from_everyone(): lax.all_to_all(jnp.broadcast_to(x[None], (length, *x.shape)), axis, 0, 0,...]
    split x1 -> x0, local copies, waits for them, and re-layouts: 11.9 us -> none  [side_by_side(): jnp.split(lax.all_gather(both, axis, axis=dim, tiled=True), ends, axis=al...]
    reduce_max x2 -> x0, other arithmetic: 3.47 us -> none  [the longest x1 3.3 us: per_device(): jnp.max(jnp.abs(latest_gained_gate), axis=0)]
  transfers between devices with their start and end apart: 1 -> 0, of which waited for: 1 -> 0; matrix products, arithmetic and copies ran while one was open for 0% -> 0% of each run, Pallas kernels for 0% -> 0%
where the time goes in v1:
time: 106 us
  Pallas kernels  105 us (99%)
    pallas_call x1, Pallas kernels, per_device(): pl.pallas_call(gather_kernel, name='ring', out_shape=(pltpu.VMEM((2, n *...  98.9 us
    pallas_call x1, Pallas kernels, per_device(): pl.pallas_call(write_kernel, name='write', out_shape=(jax.ShapeDtypeStruc...  5.99 us

profile of v1, /device:TPU:1, one launch (start us, length us, event | category | flops | bytes accessed | tf_op | source)
XLA Modules:
  0.0 106.1 jit_solution(1180822527631203122)
XLA Ops:
  0.6 0.0 copy-start
  0.6 0.6 copy-done
  1.3 98.9 %ring.1 = (bf16[2,2048,2048]{2,1,0:T(8,128)(2,1)S(1)}, f32[2,16,128]{2,1,0:T(8,128)S(1)}) custom-call(f32[128,2048]{1,0:T(8,128)} %wg.1, f32[128,2048]{1,0:T(8,128)} %mg.1, f32[128,2048]{1,0:T(8,128)} %sg.1, f32[128,2048]{1,0:T(8,128)} %wu.1, f32[128,2048]{1,0:T(8,128)} %mu.1, f32[128,2048]{1,0:T(8,128)} %su.1, f32[1,128]{1,0:T(1,128)S(1)} %bitcast.3), custom_call_target="tpu_custom_call" | custom-call | tf_op jit(solution)/shard_map/ring/pallas_call | solution.py:235
  100.1 6.0 %write.1 = (bf16[2048,2048]{1,0:T(8,128)(2,1)}, bf16[2048,2048]{1,0:T(8,128)(2,1)}, f32[16,128]{1,0:T(8,128)}, f32[16,128]{1,0:T(8,128)}) custom-call(bf16[2,2048,2048]{2,1,0:T(8,128)(2,1)S(1)} %get-tuple-element.10.full, f32[2,16,128]{2,1,0:T(8,128)S(1)} %get-tuple-element.11.fac), custom_call_target="tpu_custom_call" | custom-call | tf_op jit(solution)/shard_map/write/pallas_call | solution.py:269
Async XLA Ops:
  0.6 0.7 copy-start

commit v2 on v0

v2 whole, which is shorter than its diff:
```python
import jax
import jax.numpy as jnp
from jax import lax
from jax.experimental import pallas as pl
from jax.experimental.pallas import tpu as pltpu
from jax.sharding import PartitionSpec as P

learn_rate = 0.2
hold_rate = 0.9
MESH = pl.DeviceIdType.MESH
LANES = 128
PIECE = 512
CW, CCW = 0, 1


def gather_kernel(
    wg, mg, sg, wu, mu, su, gain_hbm, out, fac,
    buf, gain_row, gain_b, mx_own, mx_pair, mx_comb, mx_all, mx_first,
    load_sem, gain_sem, ring_send, ring_recv, pair_send, pair_recv, mxp_send, mxp_recv, mx_send, mx_recv,
    first_send, first_recv,
):
    rows, cols = wg.shape
    n_pieces = 2 * cols // PIECE
    tiles = PIECE // LANES
    chips = lax.axis_size("zero") // 2
    far_first = (4, 3, 5, 2, 6, 1, 7)

    me = lax.axis_index("zero")
    chip, core = me // 2, me % 2

    def peer(step, other=False):
        c = 1 - core if other else core
        return {"zero": lax.rem(chip + step + 2 * chips, chips) * 2 + c}

    partner = peer(0, True)

    n_groups = n_pieces // 2

    def loads(k):
        a, c = divmod(k, n_pieces // 2)
        span = pl.ds(c * PIECE, PIECE)
        dst = pl.ds(k * PIECE, PIECE)
        srcs = ((wg, mg, sg), (wu, mu, su))[a]
        return [
            pltpu.make_async_copy(src.at[:, span], buf.at[i, :, dst], load_sem.at[k])
            for i, src in enumerate(srcs)
        ]

    gain_copy = pltpu.make_async_copy(gain_hbm, gain_row, gain_sem)
    gain_copy.start()
    for k in range(n_pieces):
        for copy in loads(k):
            copy.start()

    barrier = pltpu.get_barrier_semaphore()
    for step in far_first:
        for other in (False, True):
            pl.semaphore_signal(barrier, inc=1, device_id=peer(step, other), device_id_type=MESH)
    pl.semaphore_signal(barrier, inc=1, device_id=partner, device_id_type=MESH)

    gain_copy.wait()
    gain_b[...] = jnp.broadcast_to(gain_row[...], (rows, rows)).T

    for k in range(n_pieces):
        landed = buf.at[:, :, pl.ds(k * PIECE, PIECE)]
        pltpu.make_async_copy(landed, landed, load_sem.at[k]).wait()
        for t in range(tiles):
            span = pl.ds(k * PIECE + t * LANES, LANES)
            hold = hold_rate * buf[1, :, span] + buf[2, :, span]
            gained = (buf[0, :, span] - learn_rate * hold) * gain_b[...]
            buf[0, :, span] = gained
            mx_own[k, pl.ds(t, 1), :] = jnp.max(jnp.abs(gained), axis=0, keepdims=True)

    pl.semaphore_wait(barrier, 2 * chips - 1)

    def first_copy(step, other):
        slot = 2 * step + (1 if other else 0) - 1
        return pltpu.make_async_remote_copy(
            src_ref=mx_own.at[0], dst_ref=mx_first.at[slot], send_sem=first_send,
            recv_sem=first_recv, device_id=peer(step, other), device_id_type=MESH,
        )

    direct = [(step, other) for step in far_first for other in (False, True)] + [(0, True)]
    for step, other in direct:
        first_copy(step, other).start()

    pair_max = pltpu.make_async_remote_copy(
        src_ref=mx_own.at[pl.ds(1, n_pieces - 1)], dst_ref=mx_pair, send_sem=mxp_send, recv_sem=mxp_recv,
        device_id=partner, device_id_type=MESH,
    )
    pair_max.start()
    pair_max.wait()
    mx_comb[...] = jnp.maximum(mx_own[1:], mx_pair[...])
    batches = ((0, 1), (1, 2), (3, n_pieces - 4))

    def max_copy(b, step):
        span = pl.ds(*batches[b])
        return pltpu.make_async_remote_copy(
            src_ref=mx_comb.at[span], dst_ref=mx_all.at[step - 1, span], send_sem=mx_send.at[b],
            recv_sem=mx_recv.at[b], device_id=peer(step), device_id_type=MESH,
        )

    for b in range(len(batches)):
        for step in far_first:
            max_copy(b, step).start()

    def block(way, hop, g, half):
        owner = lax.rem(chip + (2 * chips - hop if way == CW else hop), chips) * 2 + core
        width = 2 * PIECE if half is None else PIECE
        start = (g % (n_groups // 2)) * (2 * PIECE) + (half or 0) * PIECE
        rows_of = pl.ds(pl.multiple_of(owner * rows, rows), rows)
        return out.at[g // (n_groups // 2), rows_of, pl.ds(pl.multiple_of(start, PIECE), width)]

    def ring_copy(way, hop, g, half=None):
        ref = block(way, hop, g, half)
        return pltpu.make_async_remote_copy(
            src_ref=ref, dst_ref=ref, send_sem=ring_send.at[way], recv_sem=ring_recv.at[way, hop * n_groups + g],
            device_id=peer(1 if way == CW else -1), device_id_type=MESH,
        )

    def pair_copy(way, hop, g, half=None):
        ref = block(way, hop, g, half)
        return pltpu.make_async_remote_copy(
            src_ref=ref, dst_ref=ref, send_sem=pair_send, recv_sem=pair_recv, device_id=partner, device_id_type=MESH
        )

    my_rows = pl.ds(pl.multiple_of(me * rows, rows), rows)

    def send_own(k, top):
        a, c = divmod(k, n_pieces // 2)
        fac[a, pl.ds(c * tiles, tiles), :] = top
        recip = 1.0 / top
        for t in range(tiles):
            src = pl.ds(k * PIECE + t * LANES, LANES)
            dst = pl.ds(c * PIECE + t * LANES, LANES)
            out[a, my_rows, dst] = (buf[0, :, src] * recip[t : t + 1]).astype(jnp.bfloat16)
        g, half = divmod(k, 2)
        ring_copy(CW, 0, g, half).start()
        ring_copy(CCW, 0, g, half).start()
        pair_copy(CW, 0, g, half).start()

    top = mx_own[0]
    pltpu.make_async_copy(mx_first, mx_first, first_recv).wait()
    for slot in range(2 * chips - 1):
        top = jnp.maximum(top, mx_first[slot])
    send_own(0, top)
    for b, (start, size) in enumerate(batches):
        came = mx_all.at[:, pl.ds(start, size)]
        pltpu.make_async_copy(came, came, mx_recv.at[b]).wait()
        for k in range(start, start + size):
            top = mx_comb[k]
            for step in far_first:
                top = jnp.maximum(top, mx_all[step - 1, k])
            send_own(k + 1, top)

    def both(i, _):
        hop, g = i // n_groups, i % n_groups
        for way in (CW, CCW):
            ring_copy(way, hop, g).wait_recv()
            ring_copy(way, hop + 1, g).start()
            pair_copy(way, hop + 1, g).start()
        return 0

    lax.fori_loop(0, 2 * n_groups, both, 0)

    def third(g, _):
        for way in (CW, CCW):
            ring_copy(way, 2, g).wait_recv()
            ring_copy(way, 3, g, way).start()
            pair_copy(way, 3, g).start()
        return 0

    lax.fori_loop(0, n_groups, third, 0)

    def fourth(g, _):
        for way in (CW, CCW):
            ring_copy(way, 3, g, way).wait_recv()
            pair_copy(way, 4, g, way).start()
        return 0

    lax.fori_loop(0, n_groups, fourth, 0)

    theirs = out.at[:, pl.ds(0, chips * rows)]
    pltpu.make_async_copy(theirs, theirs, pair_send).wait()
    pltpu.make_async_copy(theirs, theirs, pair_recv).wait()
    for way in (CW, CCW):
        sent = out.at[0, pl.ds(0, (chips - 1) * rows)]
        pltpu.make_async_copy(sent, sent, ring_send.at[way]).wait()
    pltpu.make_async_copy(mx_first, mx_first, first_send).wait()
    for b, (start, size) in enumerate(batches):
        came = mx_all.at[:, pl.ds(start, size)]
        pltpu.make_async_copy(came, came, mx_send.at[b]).wait()


def write_kernel(full, fac, gate, up, fac_gate, fac_up, sem):
    step = full.shape[1] // 8
    smalls = [pltpu.make_async_copy(fac.at[a], dst, sem.at[2 + a]) for a, dst in enumerate((fac_gate, fac_up))]
    for a, dst in enumerate((gate, up)):
        for i in range(8):
            span = pl.ds(i * step, step)
            pltpu.make_async_copy(full.at[a, span], dst.at[span], sem.at[a]).start()
    for small in smalls:
        small.start()
    for a, dst in enumerate((gate, up)):
        pltpu.make_async_copy(full.at[a], dst, sem.at[a]).wait()
    for small in smalls:
        small.wait()


def per_device(weight_gate, moment_gate, square_gate, weight_up, moment_up, square_up, norm_gain):
    rows, cols = weight_gate.shape
    n = lax.axis_size("zero")
    chips = n // 2
    n_pieces = 2 * cols // PIECE
    tiles = PIECE // LANES
    hbm = pl.BlockSpec(memory_space=pltpu.HBM)
    vmem = pl.BlockSpec(memory_space=pltpu.VMEM)
    stored = (weight_gate, moment_gate, square_gate, weight_up, moment_up, square_up, norm_gain.reshape(1, rows))
    stored = tuple(pltpu.with_memory_space_constraint(x, pltpu.HBM) for x in stored)
    full, fac = pl.pallas_call(
        gather_kernel,
        name="ring",
        out_shape=(
            pltpu.VMEM((2, n * rows, cols), jnp.bfloat16),
            pltpu.VMEM((2, cols // LANES, LANES), jnp.float32),
        ),
        in_specs=[hbm] * 7,
        out_specs=(vmem, vmem),
        scratch_shapes=[
            pltpu.VMEM((3, rows, 2 * cols), jnp.float32),
            pltpu.VMEM((1, rows), jnp.float32),
            pltpu.VMEM((rows, rows), jnp.float32),
            pltpu.VMEM((n_pieces, tiles, LANES), jnp.float32),
            pltpu.VMEM((n_pieces - 1, tiles, LANES), jnp.float32),
            pltpu.VMEM((n_pieces - 1, tiles, LANES), jnp.float32),
            pltpu.VMEM((chips - 1, n_pieces - 1, tiles, LANES), jnp.float32),
            pltpu.VMEM((n - 1, tiles, LANES), jnp.float32),
            pltpu.SemaphoreType.DMA((n_pieces,)),
            pltpu.SemaphoreType.DMA,
            pltpu.SemaphoreType.DMA((2,)),
            pltpu.SemaphoreType.DMA((2, 2 * n_pieces)),
            pltpu.SemaphoreType.DMA,
            pltpu.SemaphoreType.DMA,
            pltpu.SemaphoreType.DMA,
            pltpu.SemaphoreType.DMA,
            pltpu.SemaphoreType.DMA((3,)),
            pltpu.SemaphoreType.DMA((3,)),
            pltpu.SemaphoreType.DMA,
            pltpu.SemaphoreType.DMA,
        ],
        compiler_params=pltpu.CompilerParams(
            collective_id=0, has_side_effects=True, vmem_limit_bytes=16 * 1024 * 1024
        ),
    )(*stored)
    full, fac = (pltpu.with_memory_space_constraint(x, pltpu.VMEM) for x in (full, fac))
    gate, up, fac_gate, fac_up = pl.pallas_call(
        write_kernel,
        name="write",
        out_shape=(
            jax.ShapeDtypeStruct((n * rows, cols), jnp.bfloat16),
            jax.ShapeDtypeStruct((n * rows, cols), jnp.bfloat16),
            jax.ShapeDtypeStruct((cols // LANES, LANES), jnp.float32),
            jax.ShapeDtypeStruct((cols // LANES, LANES), jnp.float32),
        ),
        in_specs=[pl.BlockSpec(memory_space=pl.ANY)] * 2,
        out_specs=(hbm,) * 4,
        scratch_shapes=[pltpu.SemaphoreType.DMA((4,))],
        compiler_params=pltpu.CompilerParams(vmem_limit_bytes=1024 * 1024),
    )(full, fac)
    return gate, up, fac_gate.reshape(cols), fac_up.reshape(cols)


def solution(mesh):
    placed = (P(("ens", "zero"), "cols"),) * 6 + (P(("ens", "zero")),)
    return jax.shard_map(
        per_device,
        mesh=mesh,
        in_specs=placed,
        out_specs=(P("ens", "cols"), P("ens", "cols"), P(("ens", "cols")), P(("ens", "cols"))),
        check_vma=False,
    )
```

time: 145 us -> 103 us (0.71)
  Pallas kernels: 0 us -> 102 us
  waiting for transfers between devices: 92.7 us -> 0 us
  blocking collectives: 21.4 us -> 0 us
  between operations: 14.1 us -> 0.64 us
  local copies, waits for them, and re-layouts: 12.2 us -> 0 us
  other arithmetic: 4.73 us -> 0 us
    pallas_call x0 -> x2, Pallas kernels: none -> 102 us  [the longest x1 96.2 us: per_device(): pl.pallas_call(gather_kernel, name='ring', out_shape=(pltpu.VMEM((2, n *...]
    all_gather x1 -> x0, waiting for transfers between devices: 92.7 us -> none  [side_by_side(): lax.all_gather(both, axis, axis=dim, tiled=True)]
    all_to_all x1 -> x0, blocking collectives: 21.4 us -> none  [from_everyone(): lax.all_to_all(jnp.broadcast_to(x[None], (length, *x.shape)), axis, 0, 0,...]
    split x1 -> x0, local copies, waits for them, and re-layouts: 11.9 us -> none  [side_by_side(): jnp.split(lax.all_gather(both, axis, axis=dim, tiled=True), ends, axis=al...]
    reduce_max x2 -> x0, other arithmetic: 3.47 us -> none  [the longest x1 3.3 us: per_device(): jnp.max(jnp.abs(latest_gained_gate), axis=0)]
  transfers between devices with their start and end apart: 1 -> 0, of which waited for: 1 -> 0; matrix products, arithmetic and copies ran while one was open for 0% -> 0% of each run, Pallas kernels for 0% -> 0%
where the time goes in v2:
time: 103 us
  Pallas kernels  102 us (99%)
    pallas_call x1, Pallas kernels, per_device(): pl.pallas_call(gather_kernel, name='ring', out_shape=(pltpu.VMEM((2, n *...  96.2 us
    pallas_call x1, Pallas kernels, per_device(): pl.pallas_call(write_kernel, name='write', out_shape=(jax.ShapeDtypeStruc...  5.86 us

profile of v2, /device:TPU:1, one launch (start us, length us, event | category | flops | bytes accessed | tf_op | source)
XLA Modules:
  0.0 102.7 jit_solution(9507178297136436030)
XLA Ops:
  0.6 96.2 %ring.1 = (bf16[2,2048,2048]{2,1,0:T(8,128)(2,1)S(1)}, f32[2,16,128]{2,1,0:T(8,128)S(1)}) custom-call(f32[128,2048]{1,0:T(8,128)} %wg.1, f32[128,2048]{1,0:T(8,128)} %mg.1, f32[128,2048]{1,0:T(8,128)} %sg.1, f32[128,2048]{1,0:T(8,128)} %wu.1, f32[128,2048]{1,0:T(8,128)} %mu.1, f32[128,2048]{1,0:T(8,128)} %su.1, f32[1,128]{1,0:T(1,128)} %bitcast.3), custom_call_target="tpu_custom_call" | custom-call | tf_op jit(solution)/shard_map/ring/pallas_call | solution.py:220
  96.9 5.9 %write.1 = (bf16[2048,2048]{1,0:T(8,128)(2,1)}, bf16[2048,2048]{1,0:T(8,128)(2,1)}, f32[16,128]{1,0:T(8,128)}, f32[16,128]{1,0:T(8,128)}) custom-call(bf16[2,2048,2048]{2,1,0:T(8,128)(2,1)S(1)} %get-tuple-element.10.full, f32[2,16,128]{2,1,0:T(8,128)S(1)} %get-tuple-element.11.fac), custom_call_target="tpu_custom_call" | custom-call | tf_op jit(solution)/shard_map/write/pallas_call | solution.py:256

commit v3 on v2

--- a/solution.py
+++ b/solution.py
@@ -10,14 +10,15 @@
 MESH = pl.DeviceIdType.MESH
 LANES = 128
 PIECE = 512
+EARLY = 256
 CW, CCW = 0, 1
 
 
 def gather_kernel(
     wg, mg, sg, wu, mu, su, gain_hbm, out, fac,
-    buf, gain_row, gain_b, mx_own, mx_pair, mx_comb, mx_all, mx_first,
-    load_sem, gain_sem, ring_send, ring_recv, pair_send, pair_recv, mxp_send, mxp_recv, mx_send, mx_recv,
-    first_send, first_recv,
+    buf, gain_row, gain_b, mx_own, mx_pair, mx_comb, mx_all, mx_first, mx_final, early,
+    load_sem, gain_sem, ring_send, ring_recv, pair_recv, mxp_send, mxp_recv, mx_send, mx_recv,
+    first_send, first_recv, final_send, final_recv, early_send, early_recv,
 ):
     rows, cols = wg.shape
     n_pieces = 2 * cols // PIECE
@@ -84,112 +85,186 @@
     for step, other in direct:
         first_copy(step, other).start()
 
+    share = n_pieces // 2
+    mine, theirs = core * share, (1 - core) * share
+    last = theirs + share - 1
+    early_from = pl.multiple_of(last * PIECE + PIECE - EARLY, LANES)
+
+    def early_copy(way):
+        return pltpu.make_async_remote_copy(
+            src_ref=buf.at[0, :, pl.ds(early_from, EARLY)], dst_ref=early.at[way], send_sem=early_send,
+            recv_sem=early_recv.at[way], device_id=peer(1 if way == CW else -1), device_id_type=MESH,
+        )
+
+    for way in (CW, CCW):
+        early_copy(way).start()
+
     pair_max = pltpu.make_async_remote_copy(
-        src_ref=mx_own.at[pl.ds(1, n_pieces - 1)], dst_ref=mx_pair, send_sem=mxp_send, recv_sem=mxp_recv,
+        src_ref=mx_own.at[pl.ds(theirs, share)], dst_ref=mx_pair, send_sem=mxp_send, recv_sem=mxp_recv,
         device_id=partner, device_id_type=MESH,
     )
     pair_max.start()
     pair_max.wait()
-    mx_comb[...] = jnp.maximum(mx_own[1:], mx_pair[...])
-    batches = ((0, 1), (1, 2), (3, n_pieces - 4))
+    mx_comb[...] = jnp.maximum(mx_own[pl.ds(mine, share)], mx_pair[...])
+    batch = 2
+    n_batches = share // batch
 
     def max_copy(b, step):
-        span = pl.ds(*batches[b])
-        return pltpu.make_async_remote_copy(
-            src_ref=mx_comb.at[span], dst_ref=mx_all.at[step - 1, span], send_sem=mx_send.at[b],
+        span = pl.ds(b * batch, batch)
+        return pltpu.make_async_remote_copy(
+            src_ref=mx_comb.at[span], dst_ref=mx_all.at[step - 1, span], send_sem=mx_send,
             recv_sem=mx_recv.at[b], device_id=peer(step), device_id_type=MESH,
         )
 
-    for b in range(len(batches)):
+    for b in range(n_batches):
         for step in far_first:
             max_copy(b, step).start()
 
-    def block(way, hop, g, half):
+    def part(way, hop, g, start, width):
         owner = lax.rem(chip + (2 * chips - hop if way == CW else hop), chips) * 2 + core
-        width = 2 * PIECE if half is None else PIECE
-        start = (g % (n_groups // 2)) * (2 * PIECE) + (half or 0) * PIECE
+        start = (g % (n_groups // 2)) * (2 * PIECE) + start
         rows_of = pl.ds(pl.multiple_of(owner * rows, rows), rows)
-        return out.at[g // (n_groups // 2), rows_of, pl.ds(pl.multiple_of(start, PIECE), width)]
-
-    def ring_copy(way, hop, g, half=None):
-        ref = block(way, hop, g, half)
-        return pltpu.make_async_remote_copy(
-            src_ref=ref, dst_ref=ref, send_sem=ring_send.at[way], recv_sem=ring_recv.at[way, hop * n_groups + g],
+        return out.at[g // (n_groups // 2), rows_of, pl.ds(pl.multiple_of(start, LANES), width)]
+
+    def ring_copy(way, hop, i, g, start=0, width=2 * PIECE):
+        ref = part(way, hop, g, start, width)
+        slot = hop * 2 + i // 2 if width == 2 * PIECE or hop == 0 else 6 + i
+        return pltpu.make_async_remote_copy(
+            src_ref=ref, dst_ref=ref, send_sem=ring_send, recv_sem=ring_recv.at[way, slot],
             device_id=peer(1 if way == CW else -1), device_id_type=MESH,
         )
 
-    def pair_copy(way, hop, g, half=None):
-        ref = block(way, hop, g, half)
-        return pltpu.make_async_remote_copy(
-            src_ref=ref, dst_ref=ref, send_sem=pair_send, recv_sem=pair_recv, device_id=partner, device_id_type=MESH
-        )
-
-    my_rows = pl.ds(pl.multiple_of(me * rows, rows), rows)
-
-    def send_own(k, top):
-        a, c = divmod(k, n_pieces // 2)
-        fac[a, pl.ds(c * tiles, tiles), :] = top
+    def pair_copy(way, hop, g, start=0, width=2 * PIECE):
+        ref = part(way, hop, g, start, width)
+        return pltpu.make_async_remote_copy(
+            src_ref=ref, dst_ref=ref, send_sem=ring_send, recv_sem=pair_recv, device_id=partner, device_id_type=MESH
+        )
+
+    def turn(i):
+        return lax.rem(i + core * (n_groups // 2), n_groups)
+
+    def send_own(k, i, half, top, width=PIECE):
         recip = 1.0 / top
+        a, c = k // share, k % share
         for t in range(tiles):
-            src = pl.ds(k * PIECE + t * LANES, LANES)
-            dst = pl.ds(c * PIECE + t * LANES, LANES)
-            out[a, my_rows, dst] = (buf[0, :, src] * recip[t : t + 1]).astype(jnp.bfloat16)
-        g, half = divmod(k, 2)
-        ring_copy(CW, 0, g, half).start()
-        ring_copy(CCW, 0, g, half).start()
-        pair_copy(CW, 0, g, half).start()
+            src = pl.ds(pl.multiple_of(k * PIECE + t * LANES, LANES), LANES)
+            dst = pl.ds(pl.multiple_of(c * PIECE + t * LANES, LANES), LANES)
+            rows_of = pl.ds(pl.multiple_of(me * rows, rows), rows)
+            out[a, rows_of, dst] = (buf[0, :, src] * recip[t : t + 1]).astype(jnp.bfloat16)
+        g = k // 2
+        ring_copy(CW, 0, i, g, half * PIECE, width).start()
+        ring_copy(CCW, 0, i, g, half * PIECE, width).start()
+        pair_copy(CW, 0, g, half * PIECE, PIECE).start()
 
     top = mx_own[0]
     pltpu.make_async_copy(mx_first, mx_first, first_recv).wait()
     for slot in range(2 * chips - 1):
         top = jnp.maximum(top, mx_first[slot])
-    send_own(0, top)
-    for b, (start, size) in enumerate(batches):
-        came = mx_all.at[:, pl.ds(start, size)]
+    send_own(0, core * (n_groups // 2), 0, top)
+
+    def final_copy(b):
+        ref = mx_final.at[pl.ds(mine + b * batch, batch)]
+        return pltpu.make_async_remote_copy(
+            src_ref=ref, dst_ref=ref, send_sem=final_send, recv_sem=final_recv.at[b],
+            device_id=partner, device_id_type=MESH,
+        )
+
+    for b in range(n_batches):
+        span = pl.ds(b * batch, batch)
+        came = mx_all.at[:, span]
         pltpu.make_async_copy(came, came, mx_recv.at[b]).wait()
-        for k in range(start, start + size):
-            top = mx_comb[k]
-            for step in far_first:
-                top = jnp.maximum(top, mx_all[step - 1, k])
-            send_own(k + 1, top)
-
-    def both(i, _):
-        hop, g = i // n_groups, i % n_groups
+        top = mx_comb[span]
+        for step in far_first:
+            top = jnp.maximum(top, mx_all[step - 1, span])
+        mx_final[pl.ds(mine + b * batch, batch)] = top
+        final_copy(b).start()
+        for h in range(batch):
+            if b == 0 and h == 0:
+
+                @pl.when(core == 1)
+                def _(top=top[0]):
+                    send_own(mine, 0, 0, top)
+
+            else:
+                send_own(mine + b * batch + h, b, h, top[h])
+
+    for b in range(n_batches):
+        came = mx_final.at[pl.ds(theirs + b * batch, batch)]
+        pltpu.make_async_copy(came, came, final_recv.at[b]).wait()
+        for h in range(batch):
+            k = theirs + b * batch + h
+            if b == 0 and h == 0:
+
+                @pl.when(core == 0)
+                def _(k=k):
+                    send_own(k, n_groups // 2, 0, mx_final[k])
+
+            else:
+                is_last = b == n_batches - 1 and h == batch - 1
+                send_own(k, n_groups // 2 + b, h, mx_final[k], PIECE - EARLY if is_last else PIECE)
+
+    for k in range(n_pieces):
+        a, c = divmod(k, share)
+        fac[a, pl.ds(c * tiles, tiles), :] = mx_final[k]
+
+    def landed(way, hop, pair):
+        ref = out.at[0, pl.ds(0, rows), pl.ds(0, 4 * PIECE)]
+        pltpu.make_async_copy(ref, ref, ring_recv.at[way, hop * 2 + pair]).wait()
+
+    def onward(way, hop, pair):
+        for i in (2 * pair, 2 * pair + 1):
+            g = turn(i)
+            ring_copy(way, hop + 1, i, g).start()
+            pair_copy(way, hop + 1, g).start()
+
+    for way in (CW, CCW):
+        landed(way, 0, 0)
+        onward(way, 0, 0)
+
+    recip = 1.0 / mx_final[last]
+    for way in (CW, CCW):
+        ref = out.at[0, pl.ds(0, rows - rows * EARLY // (4 * PIECE)), pl.ds(0, 4 * PIECE)]
+        pltpu.make_async_copy(ref, ref, ring_recv.at[way, 1]).wait()
+        early_copy(way).wait_recv()
+        owner = lax.rem(chip + (chips - 1 if way == CW else 1), chips) * 2 + core
+        rows_of = pl.ds(pl.multiple_of(owner * rows, rows), rows)
+        for t in range(EARLY // LANES):
+            column = (last % share) * PIECE + PIECE - EARLY + t * LANES
+            factor = recip[tiles - EARLY // LANES + t : tiles - EARLY // LANES + t + 1]
+            scaled = early[way, :, pl.ds(t * LANES, LANES)] * factor
+            out[last // share, rows_of, pl.ds(pl.multiple_of(column, LANES), LANES)] = scaled.astype(jnp.bfloat16)
+        onward(way, 0, 1)
+
+    for pair in range(2):
         for way in (CW, CCW):
-            ring_copy(way, hop, g).wait_recv()
-            ring_copy(way, hop + 1, g).start()
-            pair_copy(way, hop + 1, g).start()
+            landed(way, 1, pair)
+            onward(way, 1, pair)
+
+    for pair in range(2):
+        for way in (CW, CCW):
+            landed(way, 2, pair)
+            for i in (2 * pair, 2 * pair + 1):
+                g = turn(i)
+                ring_copy(way, 3, i, g, way * PIECE, PIECE).start()
+                pair_copy(way, 3, g).start()
+
+    def fourth(i, _):
+        g = turn(i)
+        for way in (CW, CCW):
+            ring_copy(way, 3, i, g, way * PIECE, PIECE).wait_recv()
+            pair_copy(way, 4, g, way * PIECE, PIECE).start()
         return 0
 
-    lax.fori_loop(0, 2 * n_groups, both, 0)
-
-    def third(g, _):
-        for way in (CW, CCW):
-            ring_copy(way, 2, g).wait_recv()
-            ring_copy(way, 3, g, way).start()
-            pair_copy(way, 3, g).start()
-        return 0
-
-    lax.fori_loop(0, n_groups, third, 0)
-
-    def fourth(g, _):
-        for way in (CW, CCW):
-            ring_copy(way, 3, g, way).wait_recv()
-            pair_copy(way, 4, g, way).start()
-        return 0
-
     lax.fori_loop(0, n_groups, fourth, 0)
 
-    theirs = out.at[:, pl.ds(0, chips * rows)]
-    pltpu.make_async_copy(theirs, theirs, pair_send).wait()
-    pltpu.make_async_copy(theirs, theirs, pair_recv).wait()
-    for way in (CW, CCW):
-        sent = out.at[0, pl.ds(0, (chips - 1) * rows)]
-        pltpu.make_async_copy(sent, sent, ring_send.at[way]).wait()
+    handed = out.at[:, pl.ds(0, chips * rows)]
+    pltpu.make_async_copy(handed, handed, pair_recv).wait()
+    sent = out.at[:, pl.ds(0, (2 * chips - 1) * rows - rows * EARLY // cols)]
+    pltpu.make_async_copy(sent, sent, ring_send).wait()
+    pltpu.make_async_copy(early, early, early_send).wait()
     pltpu.make_async_copy(mx_first, mx_first, first_send).wait()
-    for b, (start, size) in enumerate(batches):
-        came = mx_all.at[:, pl.ds(start, size)]
-        pltpu.make_async_copy(came, came, mx_send.at[b]).wait()
+    pltpu.make_async_copy(mx_all, mx_all, mx_send).wait()
+    pltpu.make_async_copy(mx_pair, mx_pair, final_send).wait()
 
 
 def write_kernel(full, fac, gate, up, fac_gate, fac_up, sem):
@@ -231,22 +306,27 @@
             pltpu.VMEM((1, rows), jnp.float32),
             pltpu.VMEM((rows, rows), jnp.float32),
             pltpu.VMEM((n_pieces, tiles, LANES), jnp.float32),
-            pltpu.VMEM((n_pieces - 1, tiles, LANES), jnp.float32),
-            pltpu.VMEM((n_pieces - 1, tiles, LANES), jnp.float32),
-            pltpu.VMEM((chips - 1, n_pieces - 1, tiles, LANES), jnp.float32),
+            pltpu.VMEM((n_pieces // 2, tiles, LANES), jnp.float32),
+            pltpu.VMEM((n_pieces // 2, tiles, LANES), jnp.float32),
+            pltpu.VMEM((chips - 1, n_pieces // 2, tiles, LANES), jnp.float32),
             pltpu.VMEM((n - 1, tiles, LANES), jnp.float32),
+            pltpu.VMEM((n_pieces, tiles, LANES), jnp.float32),
+            pltpu.VMEM((2, rows, EARLY), jnp.float32),
             pltpu.SemaphoreType.DMA((n_pieces,)),
             pltpu.SemaphoreType.DMA,
+            pltpu.SemaphoreType.DMA,
+            pltpu.SemaphoreType.DMA((2, 10)),
+            pltpu.SemaphoreType.DMA,
+            pltpu.SemaphoreType.DMA,
+            pltpu.SemaphoreType.DMA,
+            pltpu.SemaphoreType.DMA,
             pltpu.SemaphoreType.DMA((2,)),
-            pltpu.SemaphoreType.DMA((2, 2 * n_pieces)),
-            pltpu.SemaphoreType.DMA,
-            pltpu.SemaphoreType.DMA,
-            pltpu.SemaphoreType.DMA,
-            pltpu.SemaphoreType.DMA,
-            pltpu.SemaphoreType.DMA((3,)),
-            pltpu.SemaphoreType.DMA((3,)),
-            pltpu.SemaphoreType.DMA,
-            pltpu.SemaphoreType.DMA,
+            pltpu.SemaphoreType.DMA,
+            pltpu.SemaphoreType.DMA,
+            pltpu.SemaphoreType.DMA,
+            pltpu.SemaphoreType.DMA((2,)),
+            pltpu.SemaphoreType.DMA,
+            pltpu.SemaphoreType.DMA((2,)),
         ],
         compiler_params=pltpu.CompilerParams(
             collective_id=0, has_side_effects=True, vmem_limit_bytes=16 * 1024 * 1024

time: 103 us -> 102 us (level)
    pallas_call x1, Pallas kernels: 96.2 us -> 95 us  [per_device(): pl.pallas_call(gather_kernel, name='ring', out_shape=(pltpu.VMEM((2, n *...]
where the time goes in v3:
time: 102 us
  Pallas kernels  101 us (99%)
    pallas_call x1, Pallas kernels, per_device(): pl.pallas_call(gather_kernel, name='ring', out_shape=(pltpu.VMEM((2, n *...  95 us
    pallas_call x1, Pallas kernels, per_device(): pl.pallas_call(write_kernel, name='write', out_shape=(jax.ShapeDtypeStruc...  5.86 us

profile of v3, /device:TPU:1, one launch (start us, length us, event | category | flops | bytes accessed | tf_op | source)
XLA Modules:
  0.0 101.5 jit_solution(9644437144218672100)
XLA Ops:
  0.6 95.0 %ring.1 = (bf16[2,2048,2048]{2,1,0:T(8,128)(2,1)S(1)}, f32[2,16,128]{2,1,0:T(8,128)S(1)}) custom-call(f32[128,2048]{1,0:T(8,128)} %wg.1, f32[128,2048]{1,0:T(8,128)} %mg.1, f32[128,2048]{1,0:T(8,128)} %sg.1, f32[128,2048]{1,0:T(8,128)} %wu.1, f32[128,2048]{1,0:T(8,128)} %mu.1, f32[128,2048]{1,0:T(8,128)} %su.1, f32[1,128]{1,0:T(1,128)} %bitcast.3), custom_call_target="tpu_custom_call" | custom-call | tf_op jit(solution)/shard_map/ring/pallas_call | solution.py:295
  95.7 5.9 %write.1 = (bf16[2048,2048]{1,0:T(8,128)(2,1)}, bf16[2048,2048]{1,0:T(8,128)(2,1)}, f32[16,128]{1,0:T(8,128)}, f32[16,128]{1,0:T(8,128)}) custom-call(bf16[2,2048,2048]{2,1,0:T(8,128)(2,1)S(1)} %get-tuple-element.10.full, f32[2,16,128]{2,1,0:T(8,128)S(1)} %get-tuple-element.11.fac), custom_call_target="tpu_custom_call" | custom-call | tf_op jit(solution)/shard_map/write/pallas_call | solution.py:336

commit v4 on v3

--- a/solution.py
+++ b/solution.py
@@ -18,7 +18,7 @@
     wg, mg, sg, wu, mu, su, gain_hbm, out, fac,
     buf, gain_row, gain_b, mx_own, mx_pair, mx_comb, mx_all, mx_first, mx_final, early,
     load_sem, gain_sem, ring_send, ring_recv, pair_recv, mxp_send, mxp_recv, mx_send, mx_recv,
-    first_send, first_recv, final_send, final_recv, early_send, early_recv,
+    first_send, first_recv, final_send, final_recv, early_send, early_recv, hand_recv, relay_recv,
 ):
     rows, cols = wg.shape
     n_pieces = 2 * cols // PIECE
@@ -90,14 +90,15 @@
     last = theirs + share - 1
     early_from = pl.multiple_of(last * PIECE + PIECE - EARLY, LANES)
 
-    def early_copy(way):
-        return pltpu.make_async_remote_copy(
-            src_ref=buf.at[0, :, pl.ds(early_from, EARLY)], dst_ref=early.at[way], send_sem=early_send,
+    def early_copy(way, start, size):
+        span = pl.ds(start, size)
+        return pltpu.make_async_remote_copy(
+            src_ref=buf.at[0, span, pl.ds(early_from, EARLY)], dst_ref=early.at[way, span], send_sem=early_send,
             recv_sem=early_recv.at[way], device_id=peer(1 if way == CW else -1), device_id_type=MESH,
         )
 
     for way in (CW, CCW):
-        early_copy(way).start()
+        early_copy(way, 0, 64).start()
 
     pair_max = pltpu.make_async_remote_copy(
         src_ref=mx_own.at[pl.ds(theirs, share)], dst_ref=mx_pair, send_sem=mxp_send, recv_sem=mxp_recv,
@@ -119,6 +120,8 @@
     for b in range(n_batches):
         for step in far_first:
             max_copy(b, step).start()
+    for way in (CW, CCW):
+        early_copy(way, 64, rows - 64).start()
 
     def part(way, hop, g, start, width):
         owner = lax.rem(chip + (2 * chips - hop if way == CW else hop), chips) * 2 + core
@@ -225,7 +228,7 @@
     for way in (CW, CCW):
         ref = out.at[0, pl.ds(0, rows - rows * EARLY // (4 * PIECE)), pl.ds(0, 4 * PIECE)]
         pltpu.make_async_copy(ref, ref, ring_recv.at[way, 1]).wait()
-        early_copy(way).wait_recv()
+        pltpu.make_async_copy(early.at[way], early.at[way], early_recv.at[way]).wait()
         owner = lax.rem(chip + (chips - 1 if way == CW else 1), chips) * 2 + core
         rows_of = pl.ds(pl.multiple_of(owner * rows, rows), rows)
         for t in range(EARLY // LANES):
@@ -240,13 +243,55 @@
             landed(way, 1, pair)
             onward(way, 1, pair)
 
+    end = n_groups - 1
+
+    def handover(way):
+        ref = part(way, 3, turn(end), 0, 2 * PIECE)
+        return pltpu.make_async_remote_copy(
+            src_ref=ref, dst_ref=ref, send_sem=ring_send, recv_sem=hand_recv.at[way], device_id=partner,
+            device_id_type=MESH,
+        )
+
+    def relayed(way, hop):
+        owner = lax.rem(chip + (2 * chips - hop if way == CW else hop), chips) * 2 + 1 - core
+        g = lax.rem(end + (1 - core) * (n_groups // 2), n_groups)
+        start = (g % (n_groups // 2)) * (2 * PIECE) + way * PIECE
+        rows_of = pl.ds(pl.multiple_of(owner * rows, rows), rows)
+        return out.at[g // (n_groups // 2), rows_of, pl.ds(pl.multiple_of(start, PIECE), PIECE)]
+
+    def relay(way):
+        ref = relayed(way, 3)
+        return pltpu.make_async_remote_copy(
+            src_ref=ref, dst_ref=ref, send_sem=ring_send, recv_sem=relay_recv.at[way],
+            device_id=peer(1 if way == CW else -1), device_id_type=MESH,
+        )
+
+    def relay_back(way):
+        ref = relayed(way, 4)
+        return pltpu.make_async_remote_copy(
+            src_ref=ref, dst_ref=ref, send_sem=ring_send, recv_sem=pair_recv, device_id=partner, device_id_type=MESH
+        )
+
     for pair in range(2):
         for way in (CW, CCW):
             landed(way, 2, pair)
             for i in (2 * pair, 2 * pair + 1):
                 g = turn(i)
-                ring_copy(way, 3, i, g, way * PIECE, PIECE).start()
-                pair_copy(way, 3, g).start()
+                if i < end:
+                    ring_copy(way, 3, i, g, way * PIECE, PIECE).start()
+                    pair_copy(way, 3, g).start()
+                else:
+                    handover(way).start()
+
+                    @pl.when(core == 1)
+                    def _(way=way, i=i, g=g):
+                        ring_copy(way, 3, i, g, way * PIECE, PIECE).start()
+
+    @pl.when(core == 1)
+    def _():
+        for way in (CW, CCW):
+            handover(way).wait_recv()
+            relay(way).start()
 
     def fourth(i, _):
         g = turn(i)
@@ -255,12 +300,29 @@
             pair_copy(way, 4, g, way * PIECE, PIECE).start()
         return 0
 
-    lax.fori_loop(0, n_groups, fourth, 0)
-
-    handed = out.at[:, pl.ds(0, chips * rows)]
-    pltpu.make_async_copy(handed, handed, pair_recv).wait()
-    sent = out.at[:, pl.ds(0, (2 * chips - 1) * rows - rows * EARLY // cols)]
-    pltpu.make_async_copy(sent, sent, ring_send).wait()
+    lax.fori_loop(0, end, fourth, 0)
+
+    @pl.when(core == 1)
+    def _():
+        fourth(end, 0)
+        for way in (CW, CCW):
+            relay(way).wait_recv()
+            relay_back(way).start()
+
+
+    last_rows = rows * PIECE // cols
+    for this, sign in ((0, -1), (1, 1)):
+
+        @pl.when(core == this)
+        def _(this=this, sign=sign):
+            handed = out.at[:, pl.ds(0, chips * rows - 2 * last_rows - sign * last_rows)]
+            pltpu.make_async_copy(handed, handed, pair_recv).wait()
+            if this == 0:
+                for way in (CW, CCW):
+                    handover(way).wait_recv()
+            sent = out.at[:, pl.ds(0, (2 * chips - 1) * rows - rows * EARLY // cols + sign * 2 * last_rows)]
+            pltpu.make_async_copy(sent, sent, ring_send).wait()
+
     pltpu.make_async_copy(early, early, early_send).wait()
     pltpu.make_async_copy(mx_first, mx_first, first_send).wait()
     pltpu.make_async_copy(mx_all, mx_all, mx_send).wait()
@@ -268,10 +330,10 @@
 
 
 def write_kernel(full, fac, gate, up, fac_gate, fac_up, sem):
-    step = full.shape[1] // 8
+    step = full.shape[1] // 4
     smalls = [pltpu.make_async_copy(fac.at[a], dst, sem.at[2 + a]) for a, dst in enumerate((fac_gate, fac_up))]
     for a, dst in enumerate((gate, up)):
-        for i in range(8):
+        for i in range(4):
             span = pl.ds(i * step, step)
             pltpu.make_async_copy(full.at[a, span], dst.at[span], sem.at[a]).start()
     for small in smalls:
@@ -327,6 +389,8 @@
             pltpu.SemaphoreType.DMA((2,)),
             pltpu.SemaphoreType.DMA,
             pltpu.SemaphoreType.DMA((2,)),
+            pltpu.SemaphoreType.DMA((2,)),
+            pltpu.SemaphoreType.DMA((2,)),
         ],
         compiler_params=pltpu.CompilerParams(
             collective_id=0, has_side_effects=True, vmem_limit_bytes=16 * 1024 * 1024

time: 102 us -> 101 us (level)
  no operation moved by 1% of the time
where the time goes in v4:
time: 101 us
  Pallas kernels  100 us (99%)
    pallas_call x1, Pallas kernels, per_device(): pl.pallas_call(gather_kernel, name='ring', out_shape=(pltpu.VMEM((2, n *...  94.3 us
    pallas_call x1, Pallas kernels, per_device(): pl.pallas_call(write_kernel, name='write', out_shape=(jax.ShapeDtypeStruc...  5.89 us

profile of v4, /device:TPU:1, one launch (start us, length us, event | category | flops | bytes accessed | tf_op | source)
XLA Modules:
  0.0 100.8 jit_solution(3536487523332126988)
XLA Ops:
  0.6 94.3 %ring.1 = (bf16[2,2048,2048]{2,1,0:T(8,128)(2,1)S(1)}, f32[2,16,128]{2,1,0:T(8,128)S(1)}) custom-call(f32[128,2048]{1,0:T(8,128)} %wg.1, f32[128,2048]{1,0:T(8,128)} %mg.1, f32[128,2048]{1,0:T(8,128)} %sg.1, f32[128,2048]{1,0:T(8,128)} %wu.1, f32[128,2048]{1,0:T(8,128)} %mu.1, f32[128,2048]{1,0:T(8,128)} %su.1, f32[1,128]{1,0:T(1,128)} %bitcast.3), custom_call_target="tpu_custom_call" | custom-call | tf_op jit(solution)/shard_map/ring/pallas_call | solution.py:357
  95.0 5.9 %write.1 = (bf16[2048,2048]{1,0:T(8,128)(2,1)}, bf16[2048,2048]{1,0:T(8,128)(2,1)}, f32[16,128]{1,0:T(8,128)}, f32[16,128]{1,0:T(8,128)}) custom-call(bf16[2,2048,2048]{2,1,0:T(8,128)(2,1)S(1)} %get-tuple-element.10.full, f32[2,16,128]{2,1,0:T(8,128)S(1)} %get-tuple-element.11.fac), custom_call_target="tpu_custom_call" | custom-call | tf_op jit(solution)/shard_map/write/pallas_call | solution.py:400

commit v5 on v4

--- a/solution.py
+++ b/solution.py
@@ -10,6 +10,7 @@
 MESH = pl.DeviceIdType.MESH
 LANES = 128
 PIECE = 512
+LAST = 128
 EARLY = 256
 CW, CCW = 0, 1
 
@@ -74,37 +75,38 @@
 
     pl.semaphore_wait(barrier, 2 * chips - 1)
 
-    def first_copy(step, other):
-        slot = 2 * step + (1 if other else 0) - 1
-        return pltpu.make_async_remote_copy(
-            src_ref=mx_own.at[0], dst_ref=mx_first.at[slot], send_sem=first_send,
-            recv_sem=first_recv, device_id=peer(step, other), device_id_type=MESH,
-        )
-
-    direct = [(step, other) for step in far_first for other in (False, True)] + [(0, True)]
-    for step, other in direct:
-        first_copy(step, other).start()
-
     share = n_pieces // 2
     mine, theirs = core * share, (1 - core) * share
-    last = theirs + share - 1
-    early_from = pl.multiple_of(last * PIECE + PIECE - EARLY, LANES)
-
-    def early_copy(way, start, size):
-        span = pl.ds(start, size)
-        return pltpu.make_async_remote_copy(
-            src_ref=buf.at[0, span, pl.ds(early_from, EARLY)], dst_ref=early.at[way, span], send_sem=early_send,
-            recv_sem=early_recv.at[way], device_id=peer(1 if way == CW else -1), device_id_type=MESH,
-        )
-
-    for way in (CW, CCW):
-        early_copy(way, 0, 64).start()
-
     pair_max = pltpu.make_async_remote_copy(
         src_ref=mx_own.at[pl.ds(theirs, share)], dst_ref=mx_pair, send_sem=mxp_send, recv_sem=mxp_recv,
         device_id=partner, device_id_type=MESH,
     )
     pair_max.start()
+
+    def first_copy(step, other):
+        slot = 2 * step + (1 if other else 0) - 1
+        return pltpu.make_async_remote_copy(
+            src_ref=mx_own.at[0], dst_ref=mx_first.at[slot], send_sem=first_send,
+            recv_sem=first_recv, device_id=peer(step, other), device_id_type=MESH,
+        )
+
+    direct = [(step, other) for step in far_first for other in (False, True)] + [(0, True)]
+    for step, other in direct:
+        first_copy(step, other).start()
+
+    last = theirs + share - 1
+    early_from = pl.multiple_of(last * PIECE + PIECE - EARLY, LANES)
+
+    def early_copy(way, start, size):
+        span = pl.ds(start, size)
+        return pltpu.make_async_remote_copy(
+            src_ref=buf.at[0, span, pl.ds(early_from, EARLY)], dst_ref=early.at[way, span], send_sem=early_send,
+            recv_sem=early_recv.at[way], device_id=peer(1 if way == CW else -1), device_id_type=MESH,
+        )
+
+    for way in (CW, CCW):
+        early_copy(way, 0, 64).start()
+
     pair_max.wait()
     mx_comb[...] = jnp.maximum(mx_own[pl.ds(mine, share)], mx_pair[...])
     batch = 2
@@ -252,22 +254,29 @@
             device_id_type=MESH,
         )
 
-    def relayed(way, hop):
+    def relayed(way, hop, begin, width):
         owner = lax.rem(chip + (2 * chips - hop if way == CW else hop), chips) * 2 + 1 - core
         g = lax.rem(end + (1 - core) * (n_groups // 2), n_groups)
-        start = (g % (n_groups // 2)) * (2 * PIECE) + way * PIECE
+        start = (g % (n_groups // 2)) * (2 * PIECE) + way * PIECE + begin
         rows_of = pl.ds(pl.multiple_of(owner * rows, rows), rows)
-        return out.at[g // (n_groups // 2), rows_of, pl.ds(pl.multiple_of(start, PIECE), PIECE)]
+        return out.at[g // (n_groups // 2), rows_of, pl.ds(pl.multiple_of(start, LANES), width)]
 
     def relay(way):
-        ref = relayed(way, 3)
+        ref = relayed(way, 3, 0, PIECE - LAST)
         return pltpu.make_async_remote_copy(
             src_ref=ref, dst_ref=ref, send_sem=ring_send, recv_sem=relay_recv.at[way],
             device_id=peer(1 if way == CW else -1), device_id_type=MESH,
         )
 
+    def relay_end(way, other):
+        ref = relayed(way, 3, PIECE - LAST, LAST)
+        return pltpu.make_async_remote_copy(
+            src_ref=ref, dst_ref=ref, send_sem=ring_send, recv_sem=pair_recv,
+            device_id=peer(1 if way == CW else -1, other), device_id_type=MESH,
+        )
+
     def relay_back(way):
-        ref = relayed(way, 4)
+        ref = relayed(way, 4, 0, PIECE - LAST)
         return pltpu.make_async_remote_copy(
             src_ref=ref, dst_ref=ref, send_sem=ring_send, recv_sem=pair_recv, device_id=partner, device_id_type=MESH
         )
@@ -292,6 +301,8 @@
         for way in (CW, CCW):
             handover(way).wait_recv()
             relay(way).start()
+            relay_end(way, True).start()
+            relay_end(way, False).start()
 
     def fourth(i, _):
         g = turn(i)
@@ -315,7 +326,8 @@
 
         @pl.when(core == this)
         def _(this=this, sign=sign):
-            handed = out.at[:, pl.ds(0, chips * rows - 2 * last_rows - sign * last_rows)]
+            ends = rows * LAST // cols if this == 1 else 0
+            handed = out.at[:, pl.ds(0, chips * rows - 2 * last_rows - sign * last_rows + ends)]
             pltpu.make_async_copy(handed, handed, pair_recv).wait()
             if this == 0:
                 for way in (CW, CCW):

time: 101 us -> 100 us (0.990)
  no operation moved by 1% of the time
where the time goes in v5:
time: 100 us
  Pallas kernels  99.8 us (100%)
    pallas_call x1, Pallas kernels, per_device(): pl.pallas_call(gather_kernel, name='ring', out_shape=(pltpu.VMEM((2, n *...  93.9 us
    pallas_call x1, Pallas kernels, per_device(): pl.pallas_call(write_kernel, name='write', out_shape=(jax.ShapeDtypeStruc...  5.89 us

profile of v5, /device:TPU:1, one launch (start us, length us, event | category | flops | bytes accessed | tf_op | source)
XLA Modules:
  0.0 100.4 jit_solution(12385061696883389381)
XLA Ops:
  0.6 93.9 %ring.1 = (bf16[2,2048,2048]{2,1,0:T(8,128)(2,1)S(1)}, f32[2,16,128]{2,1,0:T(8,128)S(1)}) custom-call(f32[128,2048]{1,0:T(8,128)} %wg.1, f32[128,2048]{1,0:T(8,128)} %mg.1, f32[128,2048]{1,0:T(8,128)} %sg.1, f32[128,2048]{1,0:T(8,128)} %wu.1, f32[128,2048]{1,0:T(8,128)} %mu.1, f32[128,2048]{1,0:T(8,128)} %su.1, f32[1,128]{1,0:T(1,128)} %bitcast.3), custom_call_target="tpu_custom_call" | custom-call | tf_op jit(solution)/shard_map/ring/pallas_call | solution.py:369
  94.5 5.9 %write.1 = (bf16[2048,2048]{1,0:T(8,128)(2,1)}, bf16[2048,2048]{1,0:T(8,128)(2,1)}, f32[16,128]{1,0:T(8,128)}, f32[16,128]{1,0:T(8,128)}) custom-call(bf16[2,2048,2048]{2,1,0:T(8,128)(2,1)S(1)} %get-tuple-element.10.full, f32[2,16,128]{2,1,0:T(8,128)S(1)} %get-tuple-element.11.fac), custom_call_target="tpu_custom_call" | custom-call | tf_op jit(solution)/shard_map/write/pallas_call | solution.py:412

commit v6 on v5

--- a/solution.py
+++ b/solution.py
@@ -10,7 +10,7 @@
 MESH = pl.DeviceIdType.MESH
 LANES = 128
 PIECE = 512
-LAST = 128
+LAST = 256
 EARLY = 256
 CW, CCW = 0, 1
 

time: 100 us -> 100 us (level)
  no operation moved by 1% of the time
where the time goes in v6:
time: 100 us
  Pallas kernels  99.8 us (100%)
    pallas_call x1, Pallas kernels, per_device(): pl.pallas_call(gather_kernel, name='ring', out_shape=(pltpu.VMEM((2, n *...  93.9 us
    pallas_call x1, Pallas kernels, per_device(): pl.pallas_call(write_kernel, name='write', out_shape=(jax.ShapeDtypeStruc...  5.89 us

profile of v6, /device:TPU:1, one launch (start us, length us, event | category | flops | bytes accessed | tf_op | source)
XLA Modules:
  0.0 100.4 jit_solution(11741652425810679859)
XLA Ops:
  0.6 93.9 %ring.1 = (bf16[2,2048,2048]{2,1,0:T(8,128)(2,1)S(1)}, f32[2,16,128]{2,1,0:T(8,128)S(1)}) custom-call(f32[128,2048]{1,0:T(8,128)} %wg.1, f32[128,2048]{1,0:T(8,128)} %mg.1, f32[128,2048]{1,0:T(8,128)} %sg.1, f32[128,2048]{1,0:T(8,128)} %wu.1, f32[128,2048]{1,0:T(8,128)} %mu.1, f32[128,2048]{1,0:T(8,128)} %su.1, f32[1,128]{1,0:T(1,128)} %bitcast.3), custom_call_target="tpu_custom_call" | custom-call | tf_op jit(solution)/shard_map/ring/pallas_call | solution.py:369
  94.5 5.9 %write.1 = (bf16[2048,2048]{1,0:T(8,128)(2,1)}, bf16[2048,2048]{1,0:T(8,128)(2,1)}, f32[16,128]{1,0:T(8,128)}, f32[16,128]{1,0:T(8,128)}) custom-call(bf16[2,2048,2048]{2,1,0:T(8,128)(2,1)S(1)} %get-tuple-element.10.full, f32[2,16,128]{2,1,0:T(8,128)S(1)} %get-tuple-element.11.fac), custom_call_target="tpu_custom_call" | custom-call | tf_op jit(solution)/shard_map/write/pallas_call | solution.py:412
